TPU v7x, 32 devices: a whole 2x2x4 slice. The times are simulated.
32 devices in a mesh: tile: 8 (over z, x), sub: 4 (over y, core).
Axes of the slice: x: 2, y: 2, z: 4, core: 2. Of those that a mesh axis runs over, the one named last changes fastest.
Arguments:
- grid_feats: bfloat16 [4096, 512], P(('tile', 'sub')), may hold values from -6 to 6
- mesh_feats: bfloat16 [4096, 512], P(('tile', 'sub')), may hold values from -6 to 6
- encode_edges: bfloat16 [32768, 512], P(('tile', 'sub')), may hold values from -6 to 6
- decode_edges: bfloat16 [16384, 512], P(('tile', 'sub')), may hold values from -6 to 6
- encode_source: int32 [32768], P(('tile', 'sub')), may hold values from 0 to 4095, as said below
- encode_target: int32 [32768], P(('tile', 'sub')), may hold values from -1 to 4095, as said below
- decode_source: int32 [16384], P(('tile', 'sub')), may hold values from 0 to 4095, as said below
- decode_target: int32 [16384], P(('tile', 'sub')), may hold values from -1 to 4095, as said below
- owner_fine: int32 [4096], P(('tile', 'sub')), may hold values from 0 to 1023, as said below
- owner_coarse: int32 [1024], P('tile'), may hold values from 0 to 511
- encode_weight: bfloat16 [512, 512], replicated, may hold values from -0.25 to 0.25
- decode_weight: bfloat16 [512, 512], replicated, may hold values from -0.25 to 0.25
- middle_weight: bfloat16 [512, 512], replicated, may hold values from -0.25 to 0.25
- summit_weight: bfloat16 [512, 512], replicated, may hold values from -0.25 to 0.25
- cotangent: bfloat16 [4096, 512], P(('tile', 'sub')), may hold values from -6 to 6
Outputs:
- grid_update: bfloat16 [4096, 512], P(('tile', 'sub'))
- encode_grad: float32 [512, 512], replicated
- decode_grad: float32 [512, 512], replicated
- middle_grad: float32 [512, 512], replicated
- summit_grad: float32 [512, 512], replicated
Inputs may be any that keep to these rules, and one draw needn't show every extreme that they name: `encode_source`: edge slot e is listed on device d = e // 1024; its source grid node lies on device d - 1, d or d + 1. `encode_target`: -1 marks padding; every other value is a mesh node of the device that lists the slot. On each device padding fills whole blocks of 128 slots after all live ones; every device has a live block, and some device has no padding. `decode_source`: edge slot e is listed on device d = e // 512; its source mesh node lies on device d - 1, d or d + 1. `decode_target`: -1 marks padding; every other value is a grid node of the device that lists the slot. On each device padding fills whole blocks of 128 slots after all live ones; every device has a live block, and some device has no padding. `owner_fine`: the middle node of fine mesh node m lies on the tile of the device that holds m.
All inputs are finite; a program needn't handle non-finite values.
Results may differ from a plain program's by a relative error of at most 0.012.
Values may be sent and summed in bfloat16 or wider, within the bound.
No kernel may reach another device: no remote copies, remote signals or barrier semaphores. Data moves between devices by JAX's collectives and lax.ppermute only.
A program may use at most 64 MiB of HBM per device.

v0:
```python
import jax
import jax.numpy as jnp
from jax import lax
from jax.sharding import PartitionSpec as P

TOP_NODES = 512
BLOCK = 128


def extended(x, sides, width):
    for axis, dim in sides:
        peers, length = (lax.axis_size(axis), x.shape[dim])
        up = [(i, (i + 1) % peers) for i in range(peers - 1)]
        down = [(j, i) for i, j in up]
        last = lax.slice_in_dim(x, length - width, length, axis=dim)
        initial = lax.slice_in_dim(x, 0, width, axis=dim)
        before = lax.ppermute(last, axis, up)
        after = lax.ppermute(initial, axis, down)
        x = jnp.concatenate([before, x, after], axis=dim)
    return x


def from_behind(x, axis, by):
    peers = lax.axis_size(axis)
    pairs = [(i, i + by) for i in range(peers) if 0 <= i + by < peers]
    return lax.ppermute(x, axis, pairs)


def silu_slope(values):
    sigmoid = jax.nn.sigmoid(values)
    return sigmoid * (1.0 + values * (1.0 - sigmoid))


def live_count(targets):
    heads = targets.reshape(-1, BLOCK)[:, 0]
    return jnp.sum((heads >= 0).astype(jnp.int32))


def local_targets(targets, first, limit):
    return jnp.where(targets >= 0, targets - first, limit)


def outer_sum(left, right):
    return lax.dot_general(
        left, right, (((0,), (0,)), ((), ())), preferred_element_type=jnp.float32
    )


def times_transposed(left, right):
    return lax.dot_general(
        left, right, (((1,), (1,)), ((), ())), preferred_element_type=jnp.float32
    )


def membership(indices, rows, dtype):
    return (jnp.arange(rows, dtype=jnp.int32)[:, None] == indices[None, :]).astype(dtype)


def exact_sum(members, values):
    return jnp.dot(
        members, values, precision=lax.Precision.HIGHEST, preferred_element_type=jnp.float32
    )


def edge_forward(sources, senders, targets, edge_feats, weight, segments, blocks):
    features = weight.shape[1]

    def block_step(block_id, carried):
        summed, stored = carried
        offset = block_id * BLOCK
        picked = lax.dynamic_slice_in_dim(senders, offset, BLOCK)
        receivers = lax.dynamic_slice_in_dim(targets, offset, BLOCK)
        edge_part = lax.dynamic_slice_in_dim(edge_feats, offset, BLOCK, 0)
        fetched = jnp.take(sources, picked, axis=0)
        preact = jnp.dot(fetched, weight, preferred_element_type=jnp.float32) + edge_part.astype(
            jnp.float32
        )
        summed = summed + exact_sum(
            membership(receivers, segments, jnp.float32), jax.nn.silu(preact)
        )
        stored = lax.dynamic_update_slice_in_dim(stored, preact, offset, 0)
        return (summed, stored)

    start_sum = jnp.zeros((segments, features), jnp.float32)
    start_store = jnp.zeros((senders.shape[0], features), jnp.float32)
    return lax.fori_loop(0, blocks, block_step, (start_sum, start_store))


def edge_backward(
    sources, senders, targets, stored, weight, upstream, factor, blocks, returned_rows
):
    features = weight.shape[1]

    def block_step(block_id, carried):
        gradient, returned = carried
        offset = block_id * BLOCK
        picked = lax.dynamic_slice_in_dim(senders, offset, BLOCK)
        receivers = lax.dynamic_slice_in_dim(targets, offset, BLOCK)
        preact = lax.dynamic_slice_in_dim(stored, offset, BLOCK, 0)
        fetched = jnp.take(sources, picked, axis=0)
        incoming = jnp.take(upstream, receivers, axis=0).astype(jnp.float32) * factor
        slope = (incoming * silu_slope(preact)).astype(jnp.bfloat16)
        gradient = gradient + outer_sum(fetched, slope)
        if returned_rows:
            passed = times_transposed(slope, weight)
            returned = returned + exact_sum(membership(picked, returned_rows, jnp.float32), passed)
        return (gradient, returned)

    start_grad = jnp.zeros((features, features), jnp.float32)
    start_back = jnp.zeros((max(returned_rows, 1), features), jnp.float32)
    return lax.fori_loop(0, blocks, block_step, (start_grad, start_back))


def shards(
    grid_feats,
    mesh_feats,
    encode_edges,
    decode_edges,
    encode_source,
    encode_target,
    decode_source,
    decode_target,
    owner_fine,
    owner_coarse,
    encode_weight,
    decode_weight,
    middle_weight,
    summit_weight,
    cotangent,
):
    grid_rows = grid_feats.shape[0]
    mesh_rows = mesh_feats.shape[0]
    level_rows = owner_coarse.shape[0]
    tiles = lax.axis_size("tile")
    subs = lax.axis_size("sub")
    device = lax.axis_index(("tile", "sub"))
    tile_id = lax.axis_index("tile")
    encode_factor = mesh_rows / encode_source.shape[0]
    decode_factor = grid_rows / decode_source.shape[0]
    middle_factor = level_rows / (mesh_rows * subs)
    summit_factor = TOP_NODES / (level_rows * tiles)
    grid_wide = extended(grid_feats, ((("tile", "sub"), 0),), grid_rows)
    encode_senders = encode_source - (device - 1) * grid_rows
    encode_targets = local_targets(encode_target, device * mesh_rows, mesh_rows)
    encode_blocks = live_count(encode_target)
    encode_summed, encode_stored = edge_forward(
        grid_wide,
        encode_senders,
        encode_targets,
        encode_edges,
        encode_weight,
        mesh_rows,
        encode_blocks,
    )
    mesh_mid = (mesh_feats.astype(jnp.float32) + encode_factor * encode_summed).astype(jnp.bfloat16)
    fine_local = owner_fine - tile_id * level_rows
    fine_members = membership(fine_local, level_rows, jnp.bfloat16)
    middle_part = jnp.dot(fine_members, mesh_mid, preferred_element_type=jnp.float32)
    middle_sum = lax.psum(middle_part, "sub")
    middle_in = (middle_factor * middle_sum).astype(jnp.bfloat16)
    middle_act = jnp.dot(middle_in, middle_weight, preferred_element_type=jnp.float32)
    middle_out = (middle_in.astype(jnp.float32) + jax.nn.silu(middle_act)).astype(jnp.bfloat16)
    top_members = membership(owner_coarse, TOP_NODES, jnp.bfloat16)
    summit_part = jnp.dot(top_members, middle_out, preferred_element_type=jnp.float32)
    summit_whole = lax.psum(summit_part, "tile")
    summit_in = (summit_factor * summit_whole).astype(jnp.bfloat16)
    summit_act = jnp.dot(summit_in, summit_weight, preferred_element_type=jnp.float32)
    summit_out = jax.nn.silu(summit_act).astype(jnp.bfloat16)
    coarse_of = jnp.take(owner_coarse, fine_local)
    lifted = jnp.take(middle_out, fine_local, axis=0).astype(jnp.float32) + jnp.take(
        summit_out, coarse_of, axis=0
    ).astype(jnp.float32)
    mesh_out = (mesh_mid.astype(jnp.float32) + lifted).astype(jnp.bfloat16)
    mesh_wide = extended(mesh_out, ((("tile", "sub"), 0),), mesh_rows)
    decode_senders = decode_source - (device - 1) * mesh_rows
    decode_targets = local_targets(decode_target, device * grid_rows, grid_rows)
    decode_blocks = live_count(decode_target)
    decode_summed, decode_stored = edge_forward(
        mesh_wide,
        decode_senders,
        decode_targets,
        decode_edges,
        decode_weight,
        grid_rows,
        decode_blocks,
    )
    grid_update = (grid_feats.astype(jnp.float32) + decode_factor * decode_summed).astype(
        jnp.bfloat16
    )
    decode_local, decode_returned = edge_backward(
        mesh_wide,
        decode_senders,
        decode_targets,
        decode_stored,
        decode_weight,
        cotangent,
        decode_factor,
        decode_blocks,
        3 * mesh_rows,
    )
    from_next = from_behind(decode_returned[:mesh_rows], ("tile", "sub"), -1)
    from_prev = from_behind(decode_returned[2 * mesh_rows :], ("tile", "sub"), 1)
    mesh_grad = decode_returned[mesh_rows : 2 * mesh_rows] + from_next + from_prev
    level_part = exact_sum(fine_members.astype(jnp.float32), mesh_grad)
    level_grad = lax.psum(level_part, "sub")
    summit_grad_part = exact_sum(top_members.astype(jnp.float32), level_grad)
    summit_grad_whole = lax.psum(summit_grad_part, "tile")
    summit_slope = (summit_grad_whole * silu_slope(summit_act)).astype(jnp.bfloat16)
    summit_local = outer_sum(summit_in, summit_slope)
    summit_back = times_transposed(summit_slope, summit_weight).astype(jnp.bfloat16)
    level_total = level_grad + summit_factor * jnp.take(summit_back, owner_coarse, axis=0).astype(
        jnp.float32
    )
    middle_slope = (level_total * silu_slope(middle_act)).astype(jnp.bfloat16)
    middle_local = outer_sum(middle_in, middle_slope)
    middle_back = level_total + times_transposed(middle_slope, middle_weight)
    mesh_total = mesh_grad + middle_factor * jnp.take(middle_back, fine_local, axis=0)
    encode_local, unused_rows = edge_backward(
        grid_wide,
        encode_senders,
        encode_targets,
        encode_stored,
        encode_weight,
        mesh_total,
        encode_factor,
        encode_blocks,
        0,
    )
    sub_share = 1.0 / subs
    encode_grad, decode_grad, middle_grad = lax.psum(
        (encode_local, decode_local, sub_share * middle_local), ("tile", "sub")
    )
    return (grid_update, encode_grad, decode_grad, middle_grad, summit_local)


def solution(mesh):
    placed = (
        P(("tile", "sub"), None),
        P(("tile", "sub"), None),
        P(("tile", "sub"), None),
        P(("tile", "sub"), None),
        P(("tile", "sub")),
        P(("tile", "sub")),
        P(("tile", "sub")),
        P(("tile", "sub")),
        P(("tile", "sub")),
        P("tile"),
        P(),
        P(),
        P(),
        P(),
        P(("tile", "sub"), None),
    )
    return jax.shard_map(
        shards,
        mesh=mesh,
        in_specs=placed,
        out_specs=(P(("tile", "sub"), None), P(), P(), P(), P()),
        check_vma=False,
    )
```

profile of v0, /device:TPU:0, one launch (start us, length us, event | category | flops | bytes accessed | tf_op | source)
XLA Modules:
  0.0 564.3 jit_solution(5614955575473783883)
XLA Ops:
  7.2 2.5 collective-permute-start
  15.4 1.6 broadcast_in_dim.93
  17.0 16.3 %while.46 = (s32[]{:T(128)}, f32[128,512]{1,0:T(8,128)S(1)}, f32[1024,512]{1,0:T(8,128)}, s32[]{:T(128)}, s32[1024]{0:T(1024)S(1)}, /*index=5*/s32[1024]{0:T(102...) while((s32[]{:T(128)}, f32[128,512]{1,0:T(8,128)S(1)}, ...), condition=%wide.region_3.5_spmd, body=%wide.region_2.0_spmd.sunk | while | flops 168314624 | bytes 2367415 | solution.py:86
  18.6 1.9 constant_dynamic-update-slice_fusion.7
  22.5 1.9 constant_dynamic-update-slice_fusion.7
  26.5 1.9 constant_dynamic-update-slice_fusion.7
  30.4 1.9 constant_dynamic-update-slice_fusion.7
  34.4 52.0 %all-reduce.7.cloned.1.call-done = f32[128,512]{1,0:T(8,128)} async-done(((f32[128,512]{1,0:T(8,128)}), f32[128,512]{1,0:T(8,128)}) %all-reduce.7.cloned.1.call-update) | async-done | bytes 262160 | tf_op jit(solution)/shard_map/psum | solution.py:159
  86.4 2.0 add_convert_fusion.2
  91.9 76.8 %all-reduce.9.cloned.1.call-done = f32[512,512]{1,0:T(8,128)} async-done(((f32[512,512]{1,0:T(8,128)}), f32[512,512]{1,0:T(8,128)}) %all-reduce.9.cloned.1.call-update) | async-done | bytes 1048592 | tf_op jit(solution)/shard_map/psum | solution.py:165
  168.7 2.7 multiply_convert_fusion.6
  172.4 1.7 collective-permute-start.2
  176.7 2.0 collective-permute-done.3
  179.6 19.5 %while.47 = (s32[]{:T(128)}, f32[128,512]{1,0:T(8,128)}, f32[512,512]{1,0:T(8,128)S(1)}, s32[]{:T(128)}, s32[512]{0:T(512)}, /*index=5*/s32[512]{0:T(512)}, bf16...) while((s32[]{:T(128)}, f32[128,512]{1,0:T(8,128)}, ...), condition=%wide.region_7.10_spmd, body=%wide.region_6.9_spmd.sunk | while | flops 168314624 | bytes 2367799 | solution.py:86
  183.9 2.0 convolution_add_fusion.14
  190.1 2.0 convolution_add_fusion.14
  196.4 2.0 convolution_add_fusion.14
  200.3 22.2 %while.48 = (s32[]{:T(128)}, f32[512,512]{1,0:T(8,128)S(1)}, f32[384,512]{1,0:T(8,128)S(1)}, s32[]{:T(128)}, s32[512]{0:T(512)}, /*index=5*/bf16[384,512]{1,0:T(...) while((s32[]{:T(128)}, f32[512,512]{1,0:T(8,128)S(1)}, ...), condition=%wide.region_9.12_spmd, body=%wide.region_8.11_spmd.sunk | while | flops 438357888 | bytes 8272603 | solution.py:111
  204.1 1.5 convolution_add_fusion.15
  218.4 1.5 convolution_add_fusion.15
  223.9 6.1 %collective-permute-start.5 = (f32[128,512]{1,0:T(8,128)S(1)}, f32[128,512]{1,0:T(8,128)S(1)}, u32[]{:S(2)}, u32[]{:S(2)}) collective-permute-start(f32[128,512]{1,0:T(8,128)S(1)} %get-tuple-element.310), channel_id=1, source_target_pairs={{0,1},{1,2},{2,3},{3,4},{4,5},{5,6},{6,7},{7,8},{8,9},{9,10},{10,1... | collective-permute-start | bytes 786440 | tf_op jit(solution)/shard_map/ppermute | solution.py:26
  231.1 1.6 fusion.48
  232.8 53.1 %all-reduce.11.cloned.1.call-done = f32[128,512]{1,0:T(8,128)} async-done(((f32[128,512]{1,0:T(8,128)}), f32[128,512]{1,0:T(8,128)}) %all-reduce.11.cloned.1.call-update) | async-done | bytes 262160 | tf_op jit(solution)/shard_map/psum | solution.py:205
  285.9 2.5 fusion.42
  288.5 79.6 %all-reduce.13.cloned.1.call-done = f32[512,512]{1,0:T(8,128)} async-done(((f32[512,512]{1,0:T(8,128)}), f32[512,512]{1,0:T(8,128)}) %all-reduce.13.cloned.1.call-update) | async-done | bytes 1048592 | tf_op jit(solution)/shard_map/psum | solution.py:207
  368.1 1.9 multiply_convert_fusion.5
  371.4 1.6 convolution_add_fusion.7
  375.1 18.6 %while.49 = (s32[]{:T(128)}, f32[512,512]{1,0:T(8,128)S(1)}, s32[]{:T(128)}, s32[1024]{0:T(1024)}, bf16[384,512]{1,0:T(8,128)(2,1)S(1)}, /*index=5*/s32[1024]{0:...) while((s32[]{:T(128)}, f32[512,512]{1,0:T(8,128)S(1)}, ...), condition=%wide.region_13.16_spmd, body=%wide.region_12.15_spmd.sunk | while | flops 68161032 | bytes 3551915 | solution.py:111
  393.7 2.8 convolution_multiply_fusion
  398.2 2.7 fusion.44
  400.9 152.5 %all-reduce.15.cloned.1.call-done = (f32[512,512]{1,0:T(8,128)}, f32[512,512]{1,0:T(8,128)}, f32[512,512]{1,0:T(8,128)}) async-done(((f32[512,512]{1,0:T(8,128)}, f32[512,512]{1,0:T(8,128)}, f32[512,512]{1,0:T(8,128)}), (f32[512,512]{1,0:T(8,128)}, f32[512,512]{1,0:T(8,128)}, f32[512,512]{1,0:T(8,128)})) %all-reduce.15.cloned.1.call-update) | async-done | bytes 3145744 | tf_op jit(solution)/shard_map/psum | solution.py:230
  553.4 2.4 copy.68
  (195 shorter events, 73.4 us)
Async XLA Ops:
  7.2 161.6 %copy-start = (bf16[512,512]{1,0:T(8,128)(2,1)S(1)}, bf16[512,512]{1,0:T(8,128)(2,1)}, u32[]{:S(2)}) copy-start(bf16[512,512]{1,0:T(8,128)(2,1)} %param.40) | copy-start | bytes 1572868
  7.2 9.8 %copy-start.5 = (bf16[512,512]{1,0:T(8,128)(2,1)S(1)}, bf16[512,512]{1,0:T(8,128)(2,1)}, u32[]{:S(2)}) copy-start(bf16[512,512]{1,0:T(8,128)(2,1)} %param.37) | copy-start | bytes 1572868
  7.2 79.2 %all-reduce.7.cloned.1.call-start = ((), (), s32[]{:S(2)}) async-start(), calls=%async_computation | async-start | bytes 524288 | tf_op jit(solution)/shard_map/psum | solution.py:159
  7.2 6.5 %collective-permute-start = (bf16[128,512]{1,0:T(8,128)(2,1)}, bf16[128,512]{1,0:T(8,128)(2,1)S(1)}, u32[]{:S(2)}, u32[]{:S(2)}) collective-permute-start(bf16[128,512]{1,0:T(8,128)(2,1)} %param.27), channel_id=1, source_target_pairs={{0,1},{1,2},{2,3},{3,4},{4,5},{5,6},{6,7},{7,8},{8,9},{9,10},{10,1... | collective-permute-start | bytes 393224 | tf_op jit(solution)/shard_map/ppermute | solution.py:17
  9.8 5.6 collective-permute-start.1
  12.5 78.5 %copy-start.21 = (s32[128]{0:T(128)}, s32[128]{0:T(128)S(1)}, u32[]{:S(2)}) copy-start(s32[128]{0:T(128)S(1)} %get-tuple-element.300) | copy-start | bytes 1540
  17.0 16.4 %copy-start.14 = (bf16[128,512]{1,0:T(8,128)(2,1)S(1)}, bf16[128,512]{1,0:T(8,128)(2,1)}, u32[]{:S(2)}) copy-start(bf16[128,512]{1,0:T(8,128)(2,1)} %param.28) | copy-start | bytes 393220
  17.0 69.3 %copy-start.26 = (bf16[512,512]{1,0:T(8,128)(2,1)S(1)}, bf16[512,512]{1,0:T(8,128)(2,1)}, u32[]{:S(2)}) copy-start(bf16[512,512]{1,0:T(8,128)(2,1)} %param.39) | copy-start | bytes 1572868
  33.3 56.3 %copy-start.18 = (s32[1024]{0:T(1024)}, s32[1024]{0:T(1024)S(1)}, u32[]{:S(2)}) copy-start(s32[1024]{0:T(1024)S(1)} %get-tuple-element.780) | copy-start | bytes 12292
  33.4 56.3 %copy-start.19 = (s32[1024]{0:T(1024)}, s32[1024]{0:T(1024)S(1)}, u32[]{:S(2)}) copy-start(s32[1024]{0:T(1024)S(1)} %get-tuple-element.781) | copy-start | bytes 12292
  33.4 55.0 %copy-start.1 = (s32[128]{0:T(128)S(1)}, s32[128]{0:T(128)}, u32[]{:S(2)}) copy-start(s32[128]{0:T(128)} %param.36) | copy-start | bytes 1540
  34.3 134.4 %all-reduce.9.cloned.1.call-start = ((), (), s32[]{:S(2)}) async-start(), calls=%async_computation.1 | async-start | bytes 2097152 | tf_op jit(solution)/shard_map/psum | solution.py:165
  89.7 196.2 %all-reduce.11.cloned.1.call-start = ((), (), s32[]{:S(2)}) async-start(), calls=%async_computation.2 | async-start | bytes 524288 | tf_op jit(solution)/shard_map/psum | solution.py:205
  91.0 81.3 %copy-start.23 = (pred[128]{0:T(512)(128)(4,1)}, pred[128]{0:T(512)(128)(4,1)S(1)}, u32[]{:S(2)}) copy-start(pred[128]{0:T(512)(128)(4,1)S(1)} %get-tuple-element.298) | copy-start | bytes 388
  91.9 83.6 %copy-start.20 = (s32[512]{0:T(512)S(1)}, s32[512]{0:T(512)}, u32[]{:S(2)}) copy-start(s32[512]{0:T(512)} %param.34) | copy-start | bytes 6148
  91.9 83.6 %copy-start.25 = (s32[512]{0:T(512)S(1)}, s32[512]{0:T(512)}, u32[]{:S(2)}) copy-start(s32[512]{0:T(512)} %param.33) | copy-start | bytes 6148
  171.4 8.2 %copy-start.6 = (bf16[512,512]{1,0:T(8,128)(2,1)S(1)}, bf16[512,512]{1,0:T(8,128)(2,1)}, u32[]{:S(2)}) copy-start(bf16[512,512]{1,0:T(8,128)(2,1)} %param.38) | copy-start | bytes 1572868
  172.4 4.2 collective-permute-start.2
  174.1 4.6 collective-permute-start.3
  179.6 20.7 %copy-start.2 = (bf16[128,512]{1,0:T(8,128)(2,1)S(1)}, bf16[128,512]{1,0:T(8,128)(2,1)}, u32[]{:S(2)}) copy-start(bf16[128,512]{1,0:T(8,128)(2,1)} %param.41) | copy-start | bytes 393220
  222.5 65.9 %copy-start.3 = (f32[512,512]{1,0:T(8,128)}, f32[512,512]{1,0:T(8,128)S(1)}, u32[]{:S(2)}) copy-start(f32[512,512]{1,0:T(8,128)S(1)} %get-tuple-element.208) | copy-start | bytes 3145732
  222.6 7.4 %collective-permute-start.4 = (f32[128,512]{1,0:T(8,128)S(1)}, f32[128,512]{1,0:T(8,128)S(1)}, u32[]{:S(2)}, u32[]{:S(2)}) collective-permute-start(f32[128,512]{1,0:T(8,128)S(1)} %get-tuple-element.309), channel_id=1, source_target_pairs={{1,0},{2,1},{3,2},{4,3},{5,4},{6,5},{7,6},{8,7},{9,8},{10,9},{11,1... | collective-permute-start | bytes 786440 | tf_op jit(solution)/shard_map/ppermute | solution.py:26
  223.9 7.2 %collective-permute-start.5 = (f32[128,512]{1,0:T(8,128)S(1)}, f32[128,512]{1,0:T(8,128)S(1)}, u32[]{:S(2)}, u32[]{:S(2)}) collective-permute-start(f32[128,512]{1,0:T(8,128)S(1)} %get-tuple-element.310), channel_id=1, source_target_pairs={{0,1},{1,2},{2,3},{3,4},{4,5},{5,6},{6,7},{7,8},{8,9},{9,10},{10,1... | collective-permute-start | bytes 786440 | tf_op jit(solution)/shard_map/ppermute | solution.py:26
  231.1 138.9 %copy-start.11 = (f32[128,512]{1,0:T(8,128)}, f32[128,512]{1,0:T(8,128)S(1)}, u32[]{:S(2)}) copy-start(f32[128,512]{1,0:T(8,128)S(1)} %collective-permute-done.5) | copy-start | bytes 786436
  232.7 135.3 %all-reduce.13.cloned.1.call-start = ((), (), s32[]{:S(2)}) async-start(), calls=%async_computation.3 | async-start | bytes 2097152 | tf_op jit(solution)/shard_map/psum | solution.py:207
  288.4 264.9 %all-reduce.15.cloned.1.call-start = ((), (), s32[]{:S(2)}) async-start(), calls=%async_computation.4 | async-start | bytes 6291456 | tf_op jit(solution)/shard_map/psum | solution.py:230
  371.3 2.5 copy-start.16
  371.4 2.5 copy-start.24
  375.1 18.6 %copy-start.15 = (f32[128,512]{1,0:T(8,128)S(1)}, f32[128,512]{1,0:T(8,128)}, u32[]{:S(2)}) copy-start(f32[128,512]{1,0:T(8,128)} %all-reduce.11.cloned.1.call-done) | copy-start | bytes 786436
  375.1 18.6 %copy-start.17 = (bf16[128,512]{1,0:T(8,128)(2,1)S(1)}, bf16[128,512]{1,0:T(8,128)(2,1)}, u32[]{:S(2)}) copy-start(bf16[128,512]{1,0:T(8,128)(2,1)} %copy-done.16) | copy-start | bytes 393220
  393.7 2.8 copy-start.4
  553.4 3.4 copy-start.9
  (8 other events, 12.1 us)
Sparse Core Ops, SparseCore 0:
  34.4 51.8 all-reduce.6
  90.4 78.2 all-reduce.8
  232.9 52.9 all-reduce.10
  289.8 78.2 all-reduce.12
  396.7 156.6 all-reduce.14
where the time goes:
time: 566 us; the launch traced here: 564 us
  waiting for transfers between devices  418 us (74%)
  matrix products  53.6 us (9%)
  local copies, waits for them, and re-layouts  34.9 us (6%)
  other arithmetic  17.7 us (3%)
  starting transfers between devices  14.4 us (3%)
  between operations  14.3 us (3%)
  loops' own time  11.6 us (2%)
    psum x1, waiting for transfers between devices, shards(): lax.psum((encode_local, decode_local, sub_share * middle_local), ('tile',...  152 us
    psum x1, waiting for transfers between devices, shards(): summit_grad_whole = lax.psum(summit_grad_part, 'tile')  79.6 us
    psum x1, waiting for transfers between devices, shards(): summit_whole = lax.psum(summit_part, 'tile')  76.8 us
    psum x1, waiting for transfers between devices, shards(): level_grad = lax.psum(level_part, 'sub')  53.1 us
    psum x1, waiting for transfers between devices, shards(): middle_sum = lax.psum(middle_part, 'sub')  52 us
    dot_general x9, matrix products, outer_sum(): lax.dot_general(left, right, (((0,), (0,)), ((), ())), preferred_element_...  16 us
    dot_general x12, matrix products, exact_sum(): jnp.dot(members, values, precision=lax.Precision.HIGHEST, preferred_eleme...  13.6 us
    gather x14, local copies, waits for them, and re-layouts, block_step(): fetched = jnp.take(sources, picked, axis=0)  11.9 us
  transfers between devices with their start and end apart: 11, of which 8 were waited for; matrix products, arithmetic and copies ran while one was open for 2% of the time, Pallas kernels for 0%

commit v1 on v0

--- a/solution.py
+++ b/solution.py
@@ -202,7 +202,11 @@
     from_prev = from_behind(decode_returned[2 * mesh_rows :], ("tile", "sub"), 1)
     mesh_grad = decode_returned[mesh_rows : 2 * mesh_rows] + from_next + from_prev
     level_part = exact_sum(fine_members.astype(jnp.float32), mesh_grad)
-    level_grad = lax.psum(level_part, "sub")
+    level_grad = level_part
+    for hop in (1, 2):
+        level_grad = level_grad + lax.ppermute(
+            level_grad, "sub", [(dev, dev ^ hop) for dev in range(4)]
+        )
     summit_grad_part = exact_sum(top_members.astype(jnp.float32), level_grad)
     summit_grad_whole = lax.psum(summit_grad_part, "tile")
     summit_slope = (summit_grad_whole * silu_slope(summit_act)).astype(jnp.bfloat16)

time: 566 us -> 535 us (0.945)
  waiting for transfers between devices: 418 us -> 377 us
  starting transfers between devices: 14.4 us -> 30.3 us
  matrix products: 53.6 us -> 46.8 us
    psum x1 -> x0, waiting for transfers between devices: 53.1 us -> none  [shards(): level_grad = lax.psum(level_part, 'sub')]
    ppermute x0 -> x2, starting transfers between devices: none -> 15.9 us  [shards(): lax.ppermute(level_grad, 'sub', [(dev, dev ^ hop) for dev in range(4)])]
    ppermute x0 -> x2, waiting for transfers between devices: none -> 8 us  [shards(): lax.ppermute(level_grad, 'sub', [(dev, dev ^ hop) for dev in range(4)])]
    dot_general x12, matrix products: 13.6 us -> 7.13 us  [exact_sum(): jnp.dot(members, values, precision=lax.Precision.HIGHEST, preferred_eleme...]
  transfers between devices with their start and end apart: 11 -> 12, of which waited for: 8 -> 9; matrix products, arithmetic and copies ran while one was open for 2% -> 2% of each run, Pallas kernels for 0% -> 0%
where the time goes in v1:
time: 535 us; the launch traced here: 534 us
  waiting for transfers between devices  377 us (70%)
  matrix products  46.8 us (9%)
  local copies, waits for them, and re-layouts  34.8 us (7%)
  starting transfers between devices  30.3 us (6%)
  other arithmetic  17.8 us (3%)
  between operations  14.3 us (3%)
  loops' own time  12.1 us (2%)
    psum x1, waiting for transfers between devices, shards(): lax.psum((encode_local, decode_local, sub_share * middle_local), ('tile',...  153 us
    psum x1, waiting for transfers between devices, shards(): summit_grad_whole = lax.psum(summit_grad_part, 'tile')  83.3 us
    psum x1, waiting for transfers between devices, shards(): summit_whole = lax.psum(summit_part, 'tile')  76.8 us
    psum x1, waiting for transfers between devices, shards(): middle_sum = lax.psum(middle_part, 'sub')  52.6 us
    dot_general x9, matrix products, outer_sum(): lax.dot_general(left, right, (((0,), (0,)), ((), ())), preferred_element_...  16 us
    ppermute x2, starting transfers between devices, shards(): lax.ppermute(level_grad, 'sub', [(dev, dev ^ hop) for dev in range(4)])  15.9 us
    gather x14, local copies, waits for them, and re-layouts, block_step(): fetched = jnp.take(sources, picked, axis=0)  11.9 us
    dot_general x7, matrix products, block_step(): jnp.dot(fetched, weight, preferred_element_type=jnp.float32)  11.2 us
  transfers between devices with their start and end apart: 12, of which 9 were waited for; matrix products, arithmetic and copies ran while one was open for 2% of the time, Pallas kernels for 0%

profile of v1, /device:TPU:0, one launch (start us, length us, event | category | flops | bytes accessed | tf_op | source)
XLA Modules:
  0.0 533.6 jit_solution(1008872622091899692)
XLA Ops:
  7.2 2.5 collective-permute-start
  15.4 1.6 broadcast_in_dim.93
  17.0 16.9 %while.46 = (s32[]{:T(128)}, f32[128,512]{1,0:T(8,128)S(1)}, f32[1024,512]{1,0:T(8,128)}, s32[]{:T(128)}, s32[1024]{0:T(1024)S(1)}, /*index=5*/s32[1024]{0:T(102...) while((s32[]{:T(128)}, f32[128,512]{1,0:T(8,128)S(1)}, ...), condition=%wide.region_3.5_spmd, body=%wide.region_2.0_spmd.sunk | while | flops 168314624 | bytes 2367415 | solution.py:86
  18.7 1.9 constant_dynamic-update-slice_fusion.7
  22.8 1.9 constant_dynamic-update-slice_fusion.7
  26.8 1.9 constant_dynamic-update-slice_fusion.7
  30.8 1.9 constant_dynamic-update-slice_fusion.7
  34.9 52.6 %all-reduce.6.cloned.1.call-done = f32[128,512]{1,0:T(8,128)} async-done(((f32[128,512]{1,0:T(8,128)}), f32[128,512]{1,0:T(8,128)}) %all-reduce.6.cloned.1.call-update) | async-done | bytes 262160 | tf_op jit(solution)/shard_map/psum | solution.py:159
  87.6 2.0 add_convert_fusion.2
  93.1 76.8 %all-reduce.8.cloned.1.call-done = f32[512,512]{1,0:T(8,128)} async-done(((f32[512,512]{1,0:T(8,128)}), f32[512,512]{1,0:T(8,128)}) %all-reduce.8.cloned.1.call-update) | async-done | bytes 1048592 | tf_op jit(solution)/shard_map/psum | solution.py:165
  169.9 2.7 multiply_convert_fusion.6
  173.6 1.7 collective-permute-start.2
  177.9 2.0 collective-permute-done.3
  180.1 14.3 %while.47 = (s32[]{:T(128)}, f32[128,512]{1,0:T(8,128)S(1)}, f32[512,512]{1,0:T(8,128)S(1)}, s32[]{:T(128)}, s32[512]{0:T(512)}, /*index=5*/s32[512]{0:T(512)}, ...) while((s32[]{:T(128)}, f32[128,512]{1,0:T(8,128)S(1)}, ...), condition=%wide.region_7.10_spmd, body=%wide.region_6.9_spmd.sunk | while | flops 168314624 | bytes 2367799 | solution.py:86
  196.3 21.6 %while.48 = (s32[]{:T(128)}, f32[512,512]{1,0:T(8,128)S(1)}, f32[384,512]{1,0:T(8,128)S(1)}, s32[]{:T(128)}, s32[512]{0:T(512)}, /*index=5*/bf16[384,512]{1,0:T(...) while((s32[]{:T(128)}, f32[512,512]{1,0:T(8,128)S(1)}, ...), condition=%wide.region_9.12_spmd, body=%wide.region_8.11_spmd.sunk | while | flops 438357888 | bytes 8272603 | solution.py:111
  199.9 1.5 convolution_add_fusion.15
  206.9 1.5 convolution_add_fusion.15
  214.0 1.5 convolution_add_fusion.15
  219.3 6.1 %collective-permute-start.5 = (f32[128,512]{1,0:T(8,128)S(1)}, f32[128,512]{1,0:T(8,128)S(1)}, u32[]{:S(2)}, u32[]{:S(2)}) collective-permute-start(f32[128,512]{1,0:T(8,128)S(1)} %get-tuple-element.310), channel_id=1, source_target_pairs={{0,1},{1,2},{2,3},{3,4},{4,5},{5,6},{6,7},{7,8},{8,9},{9,10},{10,1... | collective-permute-start | bytes 786440 | tf_op jit(solution)/shard_map/ppermute | solution.py:26
  227.5 3.9 collective-permute-start.6
  232.6 12.0 %collective-permute-start.7 = (f32[128,512]{1,0:T(8,128)S(1)}, f32[128,512]{1,0:T(8,128)S(1)}, u32[]{:S(2)}, u32[]{:S(2)}) collective-permute-start(f32[128,512]{1,0:T(8,128)S(1)} %add.198), channel_id=1, source_target_pairs={{0,2},{1,3},{2,0},{3,1},{4,6},{5,7},{6,4},{7,5},{8,10},{9,11},{10,... | collective-permute-start | bytes 786440 | tf_op jit(solution)/shard_map/ppermute | solution.py:207
  244.6 6.8 %collective-permute-done.7 = f32[128,512]{1,0:T(8,128)S(1)} collective-permute-done((f32[128,512]{1,0:T(8,128)S(1)}, f32[128,512]{1,0:T(8,128)S(1)}, u32[]{:S(2)}, u32[]{:S(2)}) %collective-permute-start.7) | collective-permute-done | bytes 262176 | tf_op jit(solution)/shard_map/ppermute | solution.py:207
  251.5 1.6 fusion.42
  253.2 83.3 %all-reduce.10.cloned.1.call-done = f32[512,512]{1,0:T(8,128)} async-done(((f32[512,512]{1,0:T(8,128)}), f32[512,512]{1,0:T(8,128)}) %all-reduce.10.cloned.1.call-update) | async-done | bytes 1048592 | tf_op jit(solution)/shard_map/psum | solution.py:211
  336.5 2.0 multiply_convert_fusion.5
  343.3 19.2 %while.49 = (s32[]{:T(128)}, f32[512,512]{1,0:T(8,128)S(1)}, s32[]{:T(128)}, s32[1024]{0:T(1024)}, bf16[384,512]{1,0:T(8,128)(2,1)S(1)}, /*index=5*/s32[1024]{0:...) while((s32[]{:T(128)}, f32[512,512]{1,0:T(8,128)S(1)}, ...), condition=%wide.region_12.15_spmd, body=%wide.region_11.14_spmd.sunk | while | flops 68161032 | bytes 3551915 | solution.py:111
  351.0 1.5 convolution_add_fusion.17
  355.7 1.5 convolution_add_fusion.17
  362.5 2.8 convolution_multiply_fusion
  367.0 2.7 fusion.44
  369.7 153.0 %all-reduce.12.cloned.1.call-done = (f32[512,512]{1,0:T(8,128)}, f32[512,512]{1,0:T(8,128)}, f32[512,512]{1,0:T(8,128)}) async-done(((f32[512,512]{1,0:T(8,128)}, f32[512,512]{1,0:T(8,128)}, f32[512,512]{1,0:T(8,128)}), (f32[512,512]{1,0:T(8,128)}, f32[512,512]{1,0:T(8,128)}, f32[512,512]{1,0:T(8,128)})) %all-reduce.12.cloned.1.call-update) | async-done | bytes 3145744 | tf_op jit(solution)/shard_map/psum | solution.py:234
  522.7 2.4 copy.67
  (198 shorter events, 73.5 us)
Async XLA Ops:
  7.2 162.8 %copy-start = (bf16[512,512]{1,0:T(8,128)(2,1)S(1)}, bf16[512,512]{1,0:T(8,128)(2,1)}, u32[]{:S(2)}) copy-start(bf16[512,512]{1,0:T(8,128)(2,1)} %param.40) | copy-start | bytes 1572868
  7.2 9.8 %copy-start.5 = (bf16[512,512]{1,0:T(8,128)(2,1)S(1)}, bf16[512,512]{1,0:T(8,128)(2,1)}, u32[]{:S(2)}) copy-start(bf16[512,512]{1,0:T(8,128)(2,1)} %param.37) | copy-start | bytes 1572868
  7.2 80.4 %all-reduce.6.cloned.1.call-start = ((), (), s32[]{:S(2)}) async-start(), calls=%async_computation | async-start | bytes 524288 | tf_op jit(solution)/shard_map/psum | solution.py:159
  7.2 6.6 %collective-permute-start = (bf16[128,512]{1,0:T(8,128)(2,1)}, bf16[128,512]{1,0:T(8,128)(2,1)S(1)}, u32[]{:S(2)}, u32[]{:S(2)}) collective-permute-start(bf16[128,512]{1,0:T(8,128)(2,1)} %param.27), channel_id=1, source_target_pairs={{0,1},{1,2},{2,3},{3,4},{4,5},{5,6},{6,7},{7,8},{8,9},{9,10},{10,1... | collective-permute-start | bytes 393224 | tf_op jit(solution)/shard_map/ppermute | solution.py:17
  9.8 5.6 %collective-permute-start.1 = (bf16[128,512]{1,0:T(8,128)(2,1)}, bf16[128,512]{1,0:T(8,128)(2,1)S(1)}, u32[]{:S(2)}, u32[]{:S(2)}) collective-permute-start(bf16[128,512]{1,0:T(8,128)(2,1)} %param.27), channel_id=1, source_target_pairs={{1,0},{2,1},{3,2},{4,3},{5,4},{6,5},{7,6},{8,7},{9,8},{10,9},{11,1... | collective-permute-start | bytes 393224 | tf_op jit(solution)/shard_map/ppermute | solution.py:18
  12.5 79.7 %copy-start.20 = (s32[128]{0:T(128)}, s32[128]{0:T(128)S(1)}, u32[]{:S(2)}) copy-start(s32[128]{0:T(128)S(1)} %get-tuple-element.300) | copy-start | bytes 1540
  17.0 16.9 %copy-start.16 = (bf16[128,512]{1,0:T(8,128)(2,1)S(1)}, bf16[128,512]{1,0:T(8,128)(2,1)}, u32[]{:S(2)}) copy-start(bf16[128,512]{1,0:T(8,128)(2,1)} %param.28) | copy-start | bytes 393220
  17.0 70.5 %copy-start.25 = (bf16[512,512]{1,0:T(8,128)(2,1)S(1)}, bf16[512,512]{1,0:T(8,128)(2,1)}, u32[]{:S(2)}) copy-start(bf16[512,512]{1,0:T(8,128)(2,1)} %param.39) | copy-start | bytes 1572868
  33.9 56.9 %copy-start.17 = (s32[1024]{0:T(1024)}, s32[1024]{0:T(1024)S(1)}, u32[]{:S(2)}) copy-start(s32[1024]{0:T(1024)S(1)} %get-tuple-element.780) | copy-start | bytes 12292
  33.9 56.9 %copy-start.18 = (s32[1024]{0:T(1024)}, s32[1024]{0:T(1024)S(1)}, u32[]{:S(2)}) copy-start(s32[1024]{0:T(1024)S(1)} %get-tuple-element.781) | copy-start | bytes 12292
  33.9 55.6 %copy-start.1 = (s32[128]{0:T(128)S(1)}, s32[128]{0:T(128)}, u32[]{:S(2)}) copy-start(s32[128]{0:T(128)} %param.36) | copy-start | bytes 1540
  34.9 135.0 %all-reduce.8.cloned.1.call-start = ((), (), s32[]{:S(2)}) async-start(), calls=%async_computation.1 | async-start | bytes 2097152 | tf_op jit(solution)/shard_map/psum | solution.py:165
  90.8 245.6 %all-reduce.10.cloned.1.call-start = ((), (), s32[]{:S(2)}) async-start(), calls=%async_computation.2 | async-start | bytes 2097152 | tf_op jit(solution)/shard_map/psum | solution.py:211
  90.9 81.7 %copy-start.21 = (s32[1024]{0:T(1024)}, s32[1024]{0:T(1024)S(1)}, u32[]{:S(2)}) copy-start(s32[1024]{0:T(1024)S(1)} %pad_clamp_fusion.8) | copy-start | bytes 12292
  92.2 81.3 %copy-start.22 = (pred[128]{0:T(512)(128)(4,1)}, pred[128]{0:T(512)(128)(4,1)S(1)}, u32[]{:S(2)}) copy-start(pred[128]{0:T(512)(128)(4,1)S(1)} %get-tuple-element.298) | copy-start | bytes 388
  93.1 83.6 %copy-start.19 = (s32[512]{0:T(512)S(1)}, s32[512]{0:T(512)}, u32[]{:S(2)}) copy-start(s32[512]{0:T(512)} %param.34) | copy-start | bytes 6148
  93.1 83.6 %copy-start.24 = (s32[512]{0:T(512)S(1)}, s32[512]{0:T(512)}, u32[]{:S(2)}) copy-start(s32[512]{0:T(512)} %param.33) | copy-start | bytes 6148
  172.6 7.4 %copy-start.6 = (bf16[512,512]{1,0:T(8,128)(2,1)S(1)}, bf16[512,512]{1,0:T(8,128)(2,1)}, u32[]{:S(2)}) copy-start(bf16[512,512]{1,0:T(8,128)(2,1)} %param.38) | copy-start | bytes 1572868
  173.6 4.2 collective-permute-start.2
  175.3 4.6 collective-permute-start.3
  180.1 16.2 %copy-start.2 = (bf16[128,512]{1,0:T(8,128)(2,1)S(1)}, bf16[128,512]{1,0:T(8,128)(2,1)}, u32[]{:S(2)}) copy-start(bf16[128,512]{1,0:T(8,128)(2,1)} %param.41) | copy-start | bytes 393220
  217.9 35.1 %copy-start.3 = (f32[512,512]{1,0:T(8,128)}, f32[512,512]{1,0:T(8,128)S(1)}, u32[]{:S(2)}) copy-start(f32[512,512]{1,0:T(8,128)S(1)} %get-tuple-element.208) | copy-start | bytes 3145732
  218.0 7.4 %collective-permute-start.4 = (f32[128,512]{1,0:T(8,128)S(1)}, f32[128,512]{1,0:T(8,128)S(1)}, u32[]{:S(2)}, u32[]{:S(2)}) collective-permute-start(f32[128,512]{1,0:T(8,128)S(1)} %get-tuple-element.309), channel_id=1, source_target_pairs={{1,0},{2,1},{3,2},{4,3},{5,4},{6,5},{7,6},{8,7},{9,8},{10,9},{11,1... | collective-permute-start | bytes 786440 | tf_op jit(solution)/shard_map/ppermute | solution.py:26
  219.3 7.2 %collective-permute-start.5 = (f32[128,512]{1,0:T(8,128)S(1)}, f32[128,512]{1,0:T(8,128)S(1)}, u32[]{:S(2)}, u32[]{:S(2)}) collective-permute-start(f32[128,512]{1,0:T(8,128)S(1)} %get-tuple-element.310), channel_id=1, source_target_pairs={{0,1},{1,2},{2,3},{3,4},{4,5},{5,6},{6,7},{7,8},{8,9},{9,10},{10,1... | collective-permute-start | bytes 786440 | tf_op jit(solution)/shard_map/ppermute | solution.py:26
  225.4 6.0 %copy-start.11 = (f32[128,512]{1,0:T(8,128)}, f32[128,512]{1,0:T(8,128)S(1)}, u32[]{:S(2)}) copy-start(f32[128,512]{1,0:T(8,128)S(1)} %collective-permute-done.4) | copy-start | bytes 786436
  226.5 26.6 %copy-start.12 = (f32[128,512]{1,0:T(8,128)}, f32[128,512]{1,0:T(8,128)S(1)}, u32[]{:S(2)}) copy-start(f32[128,512]{1,0:T(8,128)S(1)} %collective-permute-done.5) | copy-start | bytes 786436
  227.5 5.1 collective-permute-start.6
  232.6 18.8 %collective-permute-start.7 = (f32[128,512]{1,0:T(8,128)S(1)}, f32[128,512]{1,0:T(8,128)S(1)}, u32[]{:S(2)}, u32[]{:S(2)}) collective-permute-start(f32[128,512]{1,0:T(8,128)S(1)} %add.198), channel_id=1, source_target_pairs={{0,2},{1,3},{2,0},{3,1},{4,6},{5,7},{6,4},{7,5},{8,10},{9,11},{10,... | collective-permute-start | bytes 786440 | tf_op jit(solution)/shard_map/ppermute | solution.py:207
  253.1 269.6 %all-reduce.12.cloned.1.call-start = ((), (), s32[]{:S(2)}) async-start(), calls=%async_computation.3 | async-start | bytes 6291456 | tf_op jit(solution)/shard_map/psum | solution.py:234
  336.4 3.3 copy-start.26
  362.5 2.8 copy-start.4
  522.7 3.4 copy-start.9
  (9 other events, 12.9 us)
Sparse Core Ops, SparseCore 0:
  35.0 52.5 all-reduce.5
  91.6 78.2 all-reduce.7
  253.2 83.1 all-reduce.9
  365.5 157.1 all-reduce.11
